TPU v7x, 32 devices: a whole 2x2x4 slice. The times are simulated.
32 devices in a mesh: layer: 8 (over y, x, core), dp: 4 (over z).
Axes of the slice: x: 2, y: 2, z: 4, core: 2. Of those that a mesh axis runs over, the one named last changes fastest.
Arguments:
- weights: bfloat16 [32, 512, 512], P('layer', 'dp'), may hold values from -0.25 to 0.25
- biases: float32 [32, 512], P('layer'), may hold values from -3 to 3
- guesses: float32 [8, 2048, 512], P('layer', 'dp'), may hold values from -6 to 6
Outputs:
- states: bfloat16 [32, 2048, 512], P('layer', 'dp')
All inputs are finite; a program needn't handle non-finite values.
Results may differ from a plain program's by a relative error of at most 0.0041.
Values may be sent and summed in bfloat16 or wider, within the bound.
No kernel may reach another device: no remote copies, remote signals or barrier semaphores. Data moves between devices by JAX's collectives and lax.ppermute only.
A program may use at most 64 MiB of HBM per device.

v0:
```python
import jax
import jax.numpy as jnp
from jax import lax
from jax.sharding import PartitionSpec as P

GROUP = 4


def from_behind(value, axis, steps):
    count = lax.axis_size(axis)
    initial, last = (max(0, -steps), min(count, count - steps))
    return lax.ppermute(value, axis, [(source, source + steps) for source in range(initial, last)])


def advance(states_in, weight_mat, bias_row, step_width):
    preact = jnp.dot(states_in.astype(jnp.bfloat16), weight_mat, preferred_element_type=jnp.float32)
    return states_in + step_width * jnp.tanh(preact + bias_row)


def take_phase(rows_all, phase):
    grouped = rows_all.reshape(rows_all.shape[0] // GROUP, GROUP, rows_all.shape[1])
    return lax.dynamic_index_in_dim(grouped, phase, 1, keepdims=False)


def put_phase(rows_all, phase, values):
    grouped = rows_all.reshape(rows_all.shape[0] // GROUP, GROUP, rows_all.shape[1])
    grouped = lax.dynamic_update_index_in_dim(grouped, values, phase, 1)
    return grouped.reshape(rows_all.shape)


def per_device(weights, biases, guesses):
    layer_count = lax.axis_size("layer")
    layer_depth = weights.shape[0]
    layer_rank = lax.axis_index("layer")
    own_phase = layer_rank % GROUP
    leader_rank = layer_rank // GROUP
    leaders = layer_count // GROUP
    fine_width = 4.0 / (layer_depth * layer_count)
    block_width = layer_depth * fine_width
    group_width = GROUP * block_width
    full_weights = lax.all_gather(weights, "dp", axis=1, tiled=True)
    head_weight = full_weights[0]
    head_bias = biases[0]
    initial = guesses[0]

    def head_step(states_in, step_width):
        return advance(states_in, head_weight, head_bias, step_width)

    current = initial
    for layer_no in range(layer_depth):
        current = advance(current, full_weights[layer_no], biases[layer_no], fine_width)
    tau_one = from_behind(current - head_step(initial, block_width), "layer", 1)
    own_guess = take_phase(initial, own_phase)
    level = initial
    carried = head_step(own_guess, group_width)
    for member in range(1, GROUP + 1):
        outgoing = head_step(take_phase(level, (layer_rank + 1 - member) % GROUP), block_width)
        incoming, carried = from_behind((outgoing, carried), "layer", 1)
        landing = (layer_rank - member) % GROUP
        moved = incoming + take_phase(tau_one, landing)
        if member < GROUP:
            level = jnp.where(layer_rank >= 1, put_phase(level, landing, moved), level)
    tau_two = moved - carried
    coarse_state = jnp.where(layer_rank == 0, own_guess, moved)

    def leader_hop(turn_no, leader_state):
        arrived = from_behind(head_step(leader_state, group_width), "layer", GROUP)
        return jnp.where(leader_rank == turn_no, arrived + tau_two, leader_state)

    coarse_state = lax.fori_loop(1, leaders, leader_hop, coarse_state)
    corrected = put_phase(initial, own_phase, coarse_state)
    for member in range(1, GROUP):
        outgoing = head_step(take_phase(corrected, (layer_rank + 1 - member) % GROUP), block_width)
        incoming = from_behind(outgoing, "layer", 1)
        landing = (layer_rank - member) % GROUP
        renewed = incoming + take_phase(tau_one, landing)
        corrected = jnp.where(layer_rank >= 1, put_phase(corrected, landing, renewed), corrected)
    outputs = []
    current = corrected
    for layer_no in range(layer_depth):
        current = advance(current, full_weights[layer_no], biases[layer_no], fine_width)
        outputs.append(current.astype(jnp.bfloat16))
    return jnp.stack(outputs)


def solution(mesh):
    in_specs = (P("layer", "dp", None), P("layer", None), P("layer", "dp", None))
    out_specs = P("layer", "dp", None)
    return jax.shard_map(
        per_device, mesh=mesh, in_specs=in_specs, out_specs=out_specs, check_vma=False
    )
```

profile of v0, /device:TPU:4, one launch (start us, length us, event | category | flops | bytes accessed | tf_op | source)
XLA Modules:
  0.0 172.4 jit_solution(7225607612104073988)
XLA Ops:
  8.1 47.7 %all-gather.2.cloned.1.call-done = bf16[4,512,512]{2,1,0:T(8,128)(2,1)} async-done(((bf16[4,128,512]{2,1,0:T(8,128)(2,1)}), bf16[4,512,512]{2,1,0:T(8,128)(2,1)}) %all-gather.2.cloned.1.call-update) | async-done | bytes 2097168 | tf_op jit(solution)/shard_map/all_gather | solution.py:41
  55.8 2.0 %fusion.22 = f32[512,512]{1,0:T(8,128)S(1)} fusion(f32[512]{0:T(512)S(1)} %bitcast.156, f32[1,512,512]{2,1,0:T(8,128)} %param.5, bf16[4,512,512]{2,1,0:T(8,128)(2,1)} %all-gather.2.cloned.1.call-done), kind=kOutput, calls=%fused_computation.31 | convolution fusion | flops 268959744 | bytes 2623488 | tf_op jit(solution)/shard_map/dot_general | solution.py:16
  58.9 1.5 fusion.15
  60.4 1.9 %collective-permute-start.1 = (f32[512,512]{1,0:T(8,128)}, f32[512,512]{1,0:T(8,128)}, u32[]{:S(2)}, u32[]{:S(2)}) collective-permute-start(f32[512,512]{1,0:T(8,128)} %fusion.15), channel_id=1, source_target_pairs={{0,4},{4,8},{8,12},{12,16},{16,20},{20,24},{24,28},{1,5},{5,9},{9,... | collective-permute-start | bytes 3145736 | tf_op jit(solution)/shard_map/ppermute | solution.py:12
  63.6 1.6 fusion.87
  67.0 3.5 %collective-permute-start = (f32[128,512]{1,0:T(8,128)}, f32[128,512]{1,0:T(8,128)}, u32[]{:S(2)}, u32[]{:S(2)}) collective-permute-start(f32[128,512]{1,0:T(8,128)} %get-tuple-element.33), channel_id=1, source_target_pairs={{0,4},{4,8},{8,12},{12,16},{16,20},{20,24},{24,28},{1,5},{5,9},{9,... | collective-permute-start | bytes 786440 | tf_op jit(solution)/shard_map/ppermute | solution.py:12
  73.1 1.9 %collective-permute-start.6 = (f32[128,512]{1,0:T(8,128)}, f32[128,512]{1,0:T(8,128)}, u32[]{:S(2)}, u32[]{:S(2)}) collective-permute-start(f32[128,512]{1,0:T(8,128)} %get-tuple-element.32), channel_id=1, source_target_pairs={{0,4},{4,8},{8,12},{12,16},{16,20},{20,24},{24,28},{1,5},{5,9},{9,... | collective-permute-start | bytes 786440 | tf_op jit(solution)/shard_map/ppermute | solution.py:12
  75.0 2.7 %collective-permute-done.1 = f32[512,512]{1,0:T(8,128)} collective-permute-done((f32[512,512]{1,0:T(8,128)}, f32[512,512]{1,0:T(8,128)}, u32[]{:S(2)}, u32[]{:S(2)}) %collective-permute-start.1) | collective-permute-done | bytes 1048608 | tf_op jit(solution)/shard_map/ppermute | solution.py:12
  77.7 2.5 %reshape.21 = f32[128,4,512]{2,1,0:T(4,128)} reshape(f32[512,512]{1,0:T(8,128)} %collective-permute-done.1) | data formatting | bytes 2097152 | tf_op jit(solution)/shard_map/reshape | solution.py:21
  80.2 4.2 %constant_dynamic-slice_fusion = (f32[128,1,512]{2,1,0:T(1,128)}, f32[128,1,512]{2,1,0:T(1,128)S(1)}, f32[128,1,512]{2,1,0:T(1,128)S(1)}, f32[128,1,512]{2,1,0:T(1,128)S(1)}) fusion(f32[128,4,512]{2,1,0:T(4,128)} %reshape.21, s32[]{:T(128)S(6)} %select_n.179, s32[]{:T(128)S(6)} %select_n.174, s32[]{:T(128)S(6)} %select_n.169, s32[]{:T(128)S(6)} %select_n.164), kind=kLoop, calls=%fused_computation.121 | loop fusion | bytes 2097168 | tf_op jit(solution)/shard_map/jit(dynamic_index_in_dim)/dynamic_slice | solution.py:22
  85.9 1.9 %collective-permute-start.2 = (f32[128,512]{1,0:T(8,128)S(1)}, f32[128,512]{1,0:T(8,128)S(1)}, u32[]{:S(2)}, u32[]{:S(2)}) collective-permute-start(f32[128,512]{1,0:T(8,128)S(1)} %fusion.46), channel_id=1, source_target_pairs={{0,4},{4,8},{8,12},{12,16},{16,20},{20,24},{24,28},{1,5},{5,9},{9,... | collective-permute-start | bytes 786440 | tf_op jit(solution)/shard_map/ppermute | solution.py:12
  87.9 2.6 %collective-permute-start.7 = (f32[128,512]{1,0:T(8,128)}, f32[128,512]{1,0:T(8,128)}, u32[]{:S(2)}, u32[]{:S(2)}) collective-permute-start(f32[128,512]{1,0:T(8,128)} %collective-permute-done.6), channel_id=1, source_target_pairs={{0,4},{4,8},{8,12},{12,16},{16,20},{20,24},{24,28},{1,5},{5,9},{9,... | collective-permute-start | bytes 786440 | tf_op jit(solution)/shard_map/ppermute | solution.py:12
  90.5 4.1 %collective-permute-done.2 = f32[128,512]{1,0:T(8,128)S(1)} collective-permute-done((f32[128,512]{1,0:T(8,128)S(1)}, f32[128,512]{1,0:T(8,128)S(1)}, u32[]{:S(2)}, u32[]{:S(2)}) %collective-permute-start.2) | collective-permute-done | bytes 262176 | tf_op jit(solution)/shard_map/ppermute | solution.py:12
  94.9 1.9 %collective-permute-start.3 = (f32[128,512]{1,0:T(8,128)S(1)}, f32[128,512]{1,0:T(8,128)S(1)}, u32[]{:S(2)}, u32[]{:S(2)}) collective-permute-start(f32[128,512]{1,0:T(8,128)S(1)} %fusion.45), channel_id=1, source_target_pairs={{0,4},{4,8},{8,12},{12,16},{16,20},{20,24},{24,28},{1,5},{5,9},{9,... | collective-permute-start | bytes 786440 | tf_op jit(solution)/shard_map/ppermute | solution.py:12
  97.4 1.9 %collective-permute-start.8 = (f32[128,512]{1,0:T(8,128)}, f32[128,512]{1,0:T(8,128)}, u32[]{:S(2)}, u32[]{:S(2)}) collective-permute-start(f32[128,512]{1,0:T(8,128)} %collective-permute-done.7), channel_id=1, source_target_pairs={{0,4},{4,8},{8,12},{12,16},{16,20},{20,24},{24,28},{1,5},{5,9},{9,... | collective-permute-start | bytes 786440 | tf_op jit(solution)/shard_map/ppermute | solution.py:12
  99.4 4.1 %collective-permute-done.3 = f32[128,512]{1,0:T(8,128)S(1)} collective-permute-done((f32[128,512]{1,0:T(8,128)S(1)}, f32[128,512]{1,0:T(8,128)S(1)}, u32[]{:S(2)}, u32[]{:S(2)}) %collective-permute-start.3) | collective-permute-done | bytes 262176 | tf_op jit(solution)/shard_map/ppermute | solution.py:12
  104.5 1.9 %collective-permute-start.4 = (f32[128,512]{1,0:T(8,128)}, f32[128,512]{1,0:T(8,128)}, u32[]{:S(2)}, u32[]{:S(2)}) collective-permute-start(f32[128,512]{1,0:T(8,128)} %fusion.44), channel_id=1, source_target_pairs={{0,4},{4,8},{8,12},{12,16},{16,20},{20,24},{24,28},{1,5},{5,9},{9,... | collective-permute-start | bytes 786440 | tf_op jit(solution)/shard_map/ppermute | solution.py:12
  106.5 1.9 %collective-permute-start.9 = (f32[128,512]{1,0:T(8,128)}, f32[128,512]{1,0:T(8,128)}, u32[]{:S(2)}, u32[]{:S(2)}) collective-permute-start(f32[128,512]{1,0:T(8,128)} %collective-permute-done.8), channel_id=1, source_target_pairs={{0,4},{4,8},{8,12},{12,16},{16,20},{20,24},{24,28},{1,5},{5,9},{9,... | collective-permute-start | bytes 786440 | tf_op jit(solution)/shard_map/ppermute | solution.py:12
  108.4 5.0 %collective-permute-done.4 = f32[128,512]{1,0:T(8,128)} collective-permute-done((f32[128,512]{1,0:T(8,128)}, f32[128,512]{1,0:T(8,128)}, u32[]{:S(2)}, u32[]{:S(2)}) %collective-permute-start.4) | collective-permute-done | bytes 262176 | tf_op jit(solution)/shard_map/ppermute | solution.py:12
  113.4 2.3 %fusion.43 = f32[128,512]{1,0:T(8,128)} fusion(f32[128,1,512]{2,1,0:T(1,128)} %copy-done.8, f32[512]{0:T(512)S(1)} %bitcast.161, pred[]{:T(512)S(6)} %eq.24, f32[128,512]{1,0:T(8,128)} %collective-permute-done.4, f32[128,1,512]{2,1,0:T(1,128)} %get-tuple-element.19, bf16[4,512,512]{2,1,0:T(8,128)(2,1)S(1)} %copy-done), kind=kOutput, calls=%fused_computation.60 | convolution fusion | flops 67633152 | bytes 2362368 | tf_op jit(solution)/shard_map/while/body/eval_jaxpr/dot_general | solution.py:16
  117.1 7.2 %collective-permute-done.5 = f32[128,512]{1,0:T(8,128)} collective-permute-done((f32[128,512]{1,0:T(8,128)}, f32[128,512]{1,0:T(8,128)}, u32[]{:S(2)}, u32[]{:S(2)}) %collective-permute-start.5) | collective-permute-done | bytes 262176 | tf_op jit(solution)/shard_map/while/body/eval_jaxpr/ppermute | solution.py:12
  126.0 1.9 %collective-permute-start.10 = (f32[128,512]{1,0:T(8,128)S(1)}, f32[128,512]{1,0:T(8,128)S(1)}, u32[]{:S(2)}, u32[]{:S(2)}) collective-permute-start(f32[128,512]{1,0:T(8,128)S(1)} %fusion.42), channel_id=1, source_target_pairs={{0,4},{4,8},{8,12},{12,16},{16,20},{20,24},{24,28},{1,5},{5,9},{9,... | collective-permute-start | bytes 786440 | tf_op jit(solution)/shard_map/ppermute | solution.py:12
  127.9 6.7 %collective-permute-done.10 = f32[128,512]{1,0:T(8,128)S(1)} collective-permute-done((f32[128,512]{1,0:T(8,128)S(1)}, f32[128,512]{1,0:T(8,128)S(1)}, u32[]{:S(2)}, u32[]{:S(2)}) %collective-permute-start.10) | collective-permute-done | bytes 262176 | tf_op jit(solution)/shard_map/ppermute | solution.py:12
  134.9 1.9 %collective-permute-start.11 = (f32[128,512]{1,0:T(8,128)S(1)}, f32[128,512]{1,0:T(8,128)S(1)}, u32[]{:S(2)}, u32[]{:S(2)}) collective-permute-start(f32[128,512]{1,0:T(8,128)S(1)} %fusion.41), channel_id=1, source_target_pairs={{0,4},{4,8},{8,12},{12,16},{16,20},{20,24},{24,28},{1,5},{5,9},{9,... | collective-permute-start | bytes 786440 | tf_op jit(solution)/shard_map/ppermute | solution.py:12
  136.8 6.7 %collective-permute-done.11 = f32[128,512]{1,0:T(8,128)S(1)} collective-permute-done((f32[128,512]{1,0:T(8,128)S(1)}, f32[128,512]{1,0:T(8,128)S(1)}, u32[]{:S(2)}, u32[]{:S(2)}) %collective-permute-start.11) | collective-permute-done | bytes 262176 | tf_op jit(solution)/shard_map/ppermute | solution.py:12
  143.8 1.9 %collective-permute-start.12 = (f32[128,512]{1,0:T(8,128)S(1)}, f32[128,512]{1,0:T(8,128)S(1)}, u32[]{:S(2)}, u32[]{:S(2)}) collective-permute-start(f32[128,512]{1,0:T(8,128)S(1)} %fusion.40), channel_id=1, source_target_pairs={{0,4},{4,8},{8,12},{12,16},{16,20},{20,24},{24,28},{1,5},{5,9},{9,... | collective-permute-start | bytes 786440 | tf_op jit(solution)/shard_map/ppermute | solution.py:12
  145.8 6.7 %collective-permute-done.12 = f32[128,512]{1,0:T(8,128)S(1)} collective-permute-done((f32[128,512]{1,0:T(8,128)S(1)}, f32[128,512]{1,0:T(8,128)S(1)}, u32[]{:S(2)}, u32[]{:S(2)}) %collective-permute-start.12) | collective-permute-done | bytes 262176 | tf_op jit(solution)/shard_map/ppermute | solution.py:12
  152.5 1.6 copy.24
  155.0 1.6 select_n.185
  156.6 2.2 %copy.25 = bf16[128,4,512]{2,1,0:T(4,128)(2,1)} copy(bf16[128,4,512]{2,0,1:T(8,128)(2,1)} %convert_element_type.105) | data formatting | bytes 1048576 | tf_op jit(solution)/shard_map/convert_element_type | solution.py:16
  158.9 2.0 %convert_element_type.106 = bf16[512,512]{1,0:T(8,128)(2,1)} reshape(bf16[128,4,512]{2,1,0:T(4,128)(2,1)} %copy.25) | data formatting | bytes 1048576 | tf_op jit(solution)/shard_map/convert_element_type | solution.py:16
  164.0 1.6 pad_maximum_fusion
  (53 shorter events, 19.3 us)
Async XLA Ops:
  6.5 51.2 %copy-start.2 = (f32[1,512,512]{2,1,0:T(8,128)S(1)}, f32[1,512,512]{2,1,0:T(8,128)}, u32[]{:S(2)}) copy-start(f32[1,512,512]{2,1,0:T(8,128)} %param.5) | copy-start | bytes 3145732
  6.5 49.3 %all-gather.2.cloned.1.call-start = ((), (), s32[]{:S(2)}) async-start(), calls=%async_computation | async-start | bytes 2621440 | tf_op jit(solution)/shard_map/all_gather | solution.py:41
  55.8 2.1 %copy-start = (bf16[4,512,512]{2,1,0:T(8,128)(2,1)S(1)}, bf16[4,512,512]{2,1,0:T(8,128)(2,1)}, u32[]{:S(2)}) copy-start(bf16[4,512,512]{2,1,0:T(8,128)(2,1)} %all-gather.2.cloned.1.call-done) | copy-start | bytes 6291460
  60.4 17.3 %collective-permute-start.1 = (f32[512,512]{1,0:T(8,128)}, f32[512,512]{1,0:T(8,128)}, u32[]{:S(2)}, u32[]{:S(2)}) collective-permute-start(f32[512,512]{1,0:T(8,128)} %fusion.15), channel_id=1, source_target_pairs={{0,4},{4,8},{8,12},{12,16},{16,20},{20,24},{24,28},{1,5},{5,9},{9,... | collective-permute-start | bytes 3145736 | tf_op jit(solution)/shard_map/ppermute | solution.py:12
  63.6 6.9 %copy-start.3 = (f32[128,4,512]{2,1,0:T(4,128)S(1)}, f32[128,4,512]{2,1,0:T(4,128)}, u32[]{:S(2)}) copy-start(f32[128,4,512]{2,1,0:T(4,128)} %reshape_squeeze.2) | copy-start | bytes 3145732
  65.3 0.7 copy-start.8
  67.0 17.4 %collective-permute-start = (f32[128,512]{1,0:T(8,128)}, f32[128,512]{1,0:T(8,128)}, u32[]{:S(2)}, u32[]{:S(2)}) collective-permute-start(f32[128,512]{1,0:T(8,128)} %get-tuple-element.33), channel_id=1, source_target_pairs={{0,4},{4,8},{8,12},{12,16},{16,20},{20,24},{24,28},{1,5},{5,9},{9,... | collective-permute-start | bytes 786440 | tf_op jit(solution)/shard_map/ppermute | solution.py:12
  73.1 14.8 %collective-permute-start.6 = (f32[128,512]{1,0:T(8,128)}, f32[128,512]{1,0:T(8,128)}, u32[]{:S(2)}, u32[]{:S(2)}) collective-permute-start(f32[128,512]{1,0:T(8,128)} %get-tuple-element.32), channel_id=1, source_target_pairs={{0,4},{4,8},{8,12},{12,16},{16,20},{20,24},{24,28},{1,5},{5,9},{9,... | collective-permute-start | bytes 786440 | tf_op jit(solution)/shard_map/ppermute | solution.py:12
  80.2 4.2 %copy-start.1 = (f32[128,4,512]{2,0,1:T(8,128)S(1)}, f32[128,4,512]{2,0,1:T(8,128)}, u32[]{:S(2)}) copy-start(f32[128,4,512]{2,0,1:T(8,128)} %copy.23) | copy-start | bytes 3145732
  84.4 10.4 %copy-start.4 = (f32[128,1,512]{2,1,0:T(1,128)}, f32[128,1,512]{2,1,0:T(1,128)S(1)}, u32[]{:S(2)}) copy-start(f32[128,1,512]{2,1,0:T(1,128)S(1)} %get-tuple-element.28) | copy-start | bytes 786436
  84.4 10.4 %copy-start.6 = (f32[128,1,512]{2,1,0:T(1,128)}, f32[128,1,512]{2,1,0:T(1,128)S(1)}, u32[]{:S(2)}) copy-start(f32[128,1,512]{2,1,0:T(1,128)S(1)} %get-tuple-element.30) | copy-start | bytes 786436
  85.9 8.6 %collective-permute-start.2 = (f32[128,512]{1,0:T(8,128)S(1)}, f32[128,512]{1,0:T(8,128)S(1)}, u32[]{:S(2)}, u32[]{:S(2)}) collective-permute-start(f32[128,512]{1,0:T(8,128)S(1)} %fusion.46), channel_id=1, source_target_pairs={{0,4},{4,8},{8,12},{12,16},{16,20},{20,24},{24,28},{1,5},{5,9},{9,... | collective-permute-start | bytes 786440 | tf_op jit(solution)/shard_map/ppermute | solution.py:12
  87.9 9.6 %collective-permute-start.7 = (f32[128,512]{1,0:T(8,128)}, f32[128,512]{1,0:T(8,128)}, u32[]{:S(2)}, u32[]{:S(2)}) collective-permute-start(f32[128,512]{1,0:T(8,128)} %collective-permute-done.6), channel_id=1, source_target_pairs={{0,4},{4,8},{8,12},{12,16},{16,20},{20,24},{24,28},{1,5},{5,9},{9,... | collective-permute-start | bytes 786440 | tf_op jit(solution)/shard_map/ppermute | solution.py:12
  94.9 8.6 %collective-permute-start.3 = (f32[128,512]{1,0:T(8,128)S(1)}, f32[128,512]{1,0:T(8,128)S(1)}, u32[]{:S(2)}, u32[]{:S(2)}) collective-permute-start(f32[128,512]{1,0:T(8,128)S(1)} %fusion.45), channel_id=1, source_target_pairs={{0,4},{4,8},{8,12},{12,16},{16,20},{20,24},{24,28},{1,5},{5,9},{9,... | collective-permute-start | bytes 786440 | tf_op jit(solution)/shard_map/ppermute | solution.py:12
  97.4 9.0 %collective-permute-start.8 = (f32[128,512]{1,0:T(8,128)}, f32[128,512]{1,0:T(8,128)}, u32[]{:S(2)}, u32[]{:S(2)}) collective-permute-start(f32[128,512]{1,0:T(8,128)} %collective-permute-done.7), channel_id=1, source_target_pairs={{0,4},{4,8},{8,12},{12,16},{16,20},{20,24},{24,28},{1,5},{5,9},{9,... | collective-permute-start | bytes 786440 | tf_op jit(solution)/shard_map/ppermute | solution.py:12
  104.5 8.9 %collective-permute-start.4 = (f32[128,512]{1,0:T(8,128)}, f32[128,512]{1,0:T(8,128)}, u32[]{:S(2)}, u32[]{:S(2)}) collective-permute-start(f32[128,512]{1,0:T(8,128)} %fusion.44), channel_id=1, source_target_pairs={{0,4},{4,8},{8,12},{12,16},{16,20},{20,24},{24,28},{1,5},{5,9},{9,... | collective-permute-start | bytes 786440 | tf_op jit(solution)/shard_map/ppermute | solution.py:12
  106.5 10.6 %collective-permute-start.9 = (f32[128,512]{1,0:T(8,128)}, f32[128,512]{1,0:T(8,128)}, u32[]{:S(2)}, u32[]{:S(2)}) collective-permute-start(f32[128,512]{1,0:T(8,128)} %collective-permute-done.8), channel_id=1, source_target_pairs={{0,4},{4,8},{8,12},{12,16},{16,20},{20,24},{24,28},{1,5},{5,9},{9,... | collective-permute-start | bytes 786440 | tf_op jit(solution)/shard_map/ppermute | solution.py:12
  115.8 8.6 %collective-permute-start.5 = (f32[128,512]{1,0:T(8,128)}, f32[128,512]{1,0:T(8,128)}, u32[]{:S(2)}, u32[]{:S(2)}) collective-permute-start(f32[128,512]{1,0:T(8,128)} %fusion.43), channel_id=1, source_target_pairs={{0,16},{4,20},{8,24},{12,28},{1,17},{5,21},{9,25},{13,29},{2,18},{... | collective-permute-start | bytes 786440 | tf_op jit(solution)/shard_map/while/body/eval_jaxpr/ppermute | solution.py:12
  117.1 17.5 %copy-start.7 = (f32[128,1,512]{2,1,0:T(1,128)S(1)}, f32[128,1,512]{2,1,0:T(1,128)}, u32[]{:S(2)}) copy-start(f32[128,1,512]{2,1,0:T(1,128)} %copy-done.6) | copy-start | bytes 786436
  125.7 17.8 %copy-start.5 = (f32[128,1,512]{2,1,0:T(1,128)S(1)}, f32[128,1,512]{2,1,0:T(1,128)}, u32[]{:S(2)}) copy-start(f32[128,1,512]{2,1,0:T(1,128)} %copy-done.4) | copy-start | bytes 786436
  126.0 8.6 %collective-permute-start.10 = (f32[128,512]{1,0:T(8,128)S(1)}, f32[128,512]{1,0:T(8,128)S(1)}, u32[]{:S(2)}, u32[]{:S(2)}) collective-permute-start(f32[128,512]{1,0:T(8,128)S(1)} %fusion.42), channel_id=1, source_target_pairs={{0,4},{4,8},{8,12},{12,16},{16,20},{20,24},{24,28},{1,5},{5,9},{9,... | collective-permute-start | bytes 786440 | tf_op jit(solution)/shard_map/ppermute | solution.py:12
  134.9 8.6 %collective-permute-start.11 = (f32[128,512]{1,0:T(8,128)S(1)}, f32[128,512]{1,0:T(8,128)S(1)}, u32[]{:S(2)}, u32[]{:S(2)}) collective-permute-start(f32[128,512]{1,0:T(8,128)S(1)} %fusion.41), channel_id=1, source_target_pairs={{0,4},{4,8},{8,12},{12,16},{16,20},{20,24},{24,28},{1,5},{5,9},{9,... | collective-permute-start | bytes 786440 | tf_op jit(solution)/shard_map/ppermute | solution.py:12
  143.8 8.6 %collective-permute-start.12 = (f32[128,512]{1,0:T(8,128)S(1)}, f32[128,512]{1,0:T(8,128)S(1)}, u32[]{:S(2)}, u32[]{:S(2)}) collective-permute-start(f32[128,512]{1,0:T(8,128)S(1)} %fusion.40), channel_id=1, source_target_pairs={{0,4},{4,8},{8,12},{12,16},{16,20},{20,24},{24,28},{1,5},{5,9},{9,... | collective-permute-start | bytes 786440 | tf_op jit(solution)/shard_map/ppermute | solution.py:12
Sparse Core Ops, SparseCore 0:
  8.9 46.8 all-gather.1
where the time goes:
time: 173 us; the launch traced here: 172 us
  waiting for transfers between devices  92.2 us (53%)
  starting transfers between devices  26.5 us (15%)
  local copies, waits for them, and re-layouts  19.6 us (11%)
  between operations  13.9 us (8%)
  matrix products  12.9 us (7%)
  other arithmetic  7.32 us (4%)
    all_gather x1, waiting for transfers between devices, per_device(): full_weights = lax.all_gather(weights, 'dp', axis=1, tiled=True)  47.7 us
    ppermute x13, waiting for transfers between devices, from_behind(): lax.ppermute(value, axis, [(source, source + steps) for source in range(i...  43.8 us
    ppermute x13, starting transfers between devices, from_behind(): lax.ppermute(value, axis, [(source, source + steps) for source in range(i...  26.5 us
    dot_general x16, matrix products, advance(): jnp.dot(states_in.astype(jnp.bfloat16), weight_mat, preferred_element_typ...  12.9 us
    convert_element_type x2, local copies, waits for them, and re-layouts, advance(): states_in.astype(jnp.bfloat16)  4.21 us
    dynamic_slice x1, local copies, waits for them, and re-layouts, take_phase(): return lax.dynamic_index_in_dim(grouped, phase, 1, keepdims=False)  4.21 us
  transfers between devices with their start and end apart: 14, of which 10 were waited for; matrix products, arithmetic and copies ran while one was open for 11% of the time, Pallas kernels for 0%

commit v1 on v0

--- a/solution.py
+++ b/solution.py
@@ -2,6 +2,7 @@
 import jax.numpy as jnp
 from jax import lax
 from jax.sharding import PartitionSpec as P
+from jax.lax import axis_index, axis_size, ppermute
 
 GROUP = 4
 
@@ -38,7 +39,16 @@
     fine_width = 4.0 / (layer_depth * layer_count)
     block_width = layer_depth * fine_width
     group_width = GROUP * block_width
-    full_weights = lax.all_gather(weights, "dp", axis=1, tiled=True)
+    size_here = axis_size("dp")
+    store = [weights]
+    for m in [*range(size_here - 1)]:
+        known = ppermute(
+            store[-1], "dp", [(src_i, (src_i + 1) % size_here) for src_i in range(size_here)]
+        )
+        store.append(known)
+    block_last = jnp.concatenate(store[::-1], 1)
+    latest = axis_index("dp")
+    full_weights = jnp.roll(block_last, (latest + 1) * weights.shape[1], 1)
     head_weight = full_weights[0]
     head_bias = biases[0]
     initial = guesses[0]

time: 173 us -> 160 us (0.925)
  between operations: 13.9 us -> 0.67 us
  matrix products: 12.9 us -> 19.7 us
  waiting for transfers between devices: 92.2 us -> 87.4 us
  other arithmetic: 7.32 us -> 3.48 us
  starting transfers between devices: 26.5 us -> 28.6 us
    all_gather x1 -> x0, waiting for transfers between devices: 47.7 us -> none  [per_device(): full_weights = lax.all_gather(weights, 'dp', axis=1, tiled=True)]
    ppermute x0 -> x3, waiting for transfers between devices: none -> 40.8 us  [per_device(): ppermute(store[-1], 'dp', [(src_i, (src_i + 1) % size_here) for src_i in...]
    dot_general x16, matrix products: 12.9 us -> 19.7 us  [advance(): jnp.dot(states_in.astype(jnp.bfloat16), weight_mat, preferred_element_typ...]
    unnamed x19 -> x29, local copies, waits for them, and re-layouts: 2.03 us -> 6.31 us
    ppermute x13, waiting for transfers between devices: 43.8 us -> 46.5 us  [from_behind(): lax.ppermute(value, axis, [(source, source + steps) for source in range(i...]
    convert_element_type x2, local copies, waits for them, and re-layouts: 4.21 us -> 1.58 us  [advance(): states_in.astype(jnp.bfloat16)]
    dynamic_slice x1, local copies, waits for them, and re-layouts: 4.21 us -> 1.61 us  [take_phase(): return lax.dynamic_index_in_dim(grouped, phase, 1, keepdims=False)]
    ppermute x0 -> x1, local copies, waits for them, and re-layouts: none -> 2.53 us  [from_behind(): lax.ppermute(value, axis, [(source, source + steps) for source in range(i...]
  transfers between devices with their start and end apart: 14 -> 16, of which waited for: 10 -> 12; matrix products, arithmetic and copies ran while one was open for 11% -> 11% of each run, Pallas kernels for 0% -> 0%
where the time goes in v1:
time: 160 us; the launch traced here: 159 us
  waiting for transfers between devices  87.4 us (55%)
  starting transfers between devices  28.6 us (18%)
  matrix products  19.7 us (12%)
  local copies, waits for them, and re-layouts  18.8 us (12%)
  other arithmetic  3.48 us (2%)
    ppermute x13, waiting for transfers between devices, from_behind(): lax.ppermute(value, axis, [(source, source + steps) for source in range(i...  46.5 us
    ppermute x3, waiting for transfers between devices, per_device(): ppermute(store[-1], 'dp', [(src_i, (src_i + 1) % size_here) for src_i in...  40.8 us
    ppermute x13, starting transfers between devices, from_behind(): lax.ppermute(value, axis, [(source, source + steps) for source in range(i...  27 us
    dot_general x16, matrix products, advance(): jnp.dot(states_in.astype(jnp.bfloat16), weight_mat, preferred_element_typ...  19.7 us
    unnamed x29, local copies, waits for them, and re-layouts  6.31 us
  transfers between devices with their start and end apart: 16, of which 12 were waited for; matrix products, arithmetic and copies ran while one was open for 11% of the time, Pallas kernels for 0%

profile of v1, /device:TPU:4, one launch (start us, length us, event | category | flops | bytes accessed | tf_op | source)
XLA Modules:
  0.0 158.7 jit_solution(5620941228953129687)
XLA Ops:
  0.0 1.6 collective-permute-start
  1.6 14.2 %collective-permute-done = bf16[4,128,512]{2,1,0:T(8,128)(2,1)S(1)} collective-permute-done((bf16[4,128,512]{2,1,0:T(8,128)(2,1)}, bf16[4,128,512]{2,1,0:T(8,128)(2,1)S(1)}, u32[]{:S(2)}, u32[]{:S(2)}) %collective-permute-start) | collective-permute-done | bytes 524320 | tf_op jit(solution)/shard_map/ppermute | solution.py:45
  15.8 14.8 %collective-permute-done.1 = bf16[4,128,512]{2,1,0:T(8,128)(2,1)} collective-permute-done((bf16[4,128,512]{2,1,0:T(8,128)(2,1)S(1)}, bf16[4,128,512]{2,1,0:T(8,128)(2,1)}, u32[]{:S(2)}, u32[]{:S(2)}) %collective-permute-start.1) | collective-permute-done | bytes 524320 | tf_op jit(solution)/shard_map/ppermute | solution.py:45
  33.1 11.8 %collective-permute-done.2 = bf16[4,128,512]{2,1,0:T(8,128)(2,1)} collective-permute-done((bf16[4,128,512]{2,1,0:T(8,128)(2,1)}, bf16[4,128,512]{2,1,0:T(8,128)(2,1)}, u32[]{:S(2)}, u32[]{:S(2)}) %collective-permute-start.2) | collective-permute-done | bytes 524320 | tf_op jit(solution)/shard_map/ppermute | solution.py:45
  52.0 1.9 %collective-permute-start.4 = (f32[512,512]{0,1:T(8,128)S(1)}, f32[512,512]{0,1:T(8,128)}, u32[]{:S(2)}, u32[]{:S(2)}) collective-permute-start(f32[512,512]{0,1:T(8,128)S(1)} %fusion.15), channel_id=1, source_target_pairs={{0,4},{4,8},{8,12},{12,16},{16,20},{20,24},{24,28},{1,5},{5,9},{9,... | collective-permute-start | bytes 3145736 | tf_op jit(solution)/shard_map/ppermute | solution.py:13
  54.6 2.1 %bitcast_add_fusion.10 = (f32[128,512]{1,0:T(8,128)}, f32[128,512]{1,0:T(8,128)}) fusion(f32[128,1,512]{2,1,0:T(1,128)S(1)} %get-tuple-element.18, f32[512]{0:T(512)S(1)} %bitcast.204, bf16[4,1024,512]{2,1,0:T(8,128)(2,1)} %copy-done, s32[]{:T(128)S(6)} %select_n.176, bf16[128,1,512]{2,1,0:T(2,128)(2,1)S(1)} %get-tuple-element.17), kind=kOutput, calls=%fused_computation.100 | convolution fusion | flops 67436544 | bytes 1443844 | tf_op jit(solution)/shard_map/dot_general | solution.py:17
  56.7 3.5 %collective-permute-start.3 = (f32[128,512]{1,0:T(8,128)}, f32[128,512]{1,0:T(8,128)}, u32[]{:S(2)}, u32[]{:S(2)}) collective-permute-start(f32[128,512]{1,0:T(8,128)} %get-tuple-element.33), channel_id=1, source_target_pairs={{0,4},{4,8},{8,12},{12,16},{16,20},{20,24},{24,28},{1,5},{5,9},{9,... | collective-permute-start | bytes 786440 | tf_op jit(solution)/shard_map/ppermute | solution.py:13
  60.7 1.9 %collective-permute-start.9 = (f32[128,512]{1,0:T(8,128)}, f32[128,512]{1,0:T(8,128)}, u32[]{:S(2)}, u32[]{:S(2)}) collective-permute-start(f32[128,512]{1,0:T(8,128)} %get-tuple-element.32), channel_id=1, source_target_pairs={{0,4},{4,8},{8,12},{12,16},{16,20},{20,24},{24,28},{1,5},{5,9},{9,... | collective-permute-start | bytes 786440 | tf_op jit(solution)/shard_map/ppermute | solution.py:13
  62.6 6.5 %collective-permute-done.4 = f32[512,512]{0,1:T(8,128)} collective-permute-done((f32[512,512]{0,1:T(8,128)S(1)}, f32[512,512]{0,1:T(8,128)}, u32[]{:S(2)}, u32[]{:S(2)}) %collective-permute-start.4) | collective-permute-done | bytes 1048608 | tf_op jit(solution)/shard_map/ppermute | solution.py:13
  69.1 2.5 %copy.40 = f32[512,512]{1,0:T(8,128)} copy(f32[512,512]{0,1:T(8,128)} %collective-permute-done.4) | data formatting | bytes 2097152 | tf_op jit(solution)/shard_map/ppermute | solution.py:13
  73.1 1.6 %constant_dynamic-slice_fusion = (f32[128,1,512]{2,1,0:T(1,128)}, f32[128,1,512]{2,1,0:T(1,128)S(1)}, f32[128,1,512]{2,1,0:T(1,128)S(1)}, f32[128,1,512]{2,1,0:T(1,128)S(1)}) fusion(f32[128,4,512]{2,1,0:T(4,128)S(1)} %reshape.21, s32[]{:T(128)S(6)} %select_n.193, s32[]{:T(128)S(6)} %select_n.188, s32[]{:T(128)S(6)} %select_n.183, s32[]{:T(128)S(6)} %select_n.178), kind=kLoop, calls=%fused_computation.141 | loop fusion | bytes 2097168 | tf_op jit(solution)/shard_map/jit(dynamic_index_in_dim)/dynamic_slice | solution.py:23
  77.4 1.9 %collective-permute-start.5 = (f32[128,512]{1,0:T(8,128)S(1)}, f32[128,512]{1,0:T(8,128)S(1)}, u32[]{:S(2)}, u32[]{:S(2)}) collective-permute-start(f32[128,512]{1,0:T(8,128)S(1)} %fusion.46), channel_id=1, source_target_pairs={{0,4},{4,8},{8,12},{12,16},{16,20},{20,24},{24,28},{1,5},{5,9},{9,... | collective-permute-start | bytes 786440 | tf_op jit(solution)/shard_map/ppermute | solution.py:13
  79.3 2.6 %collective-permute-start.10 = (f32[128,512]{1,0:T(8,128)}, f32[128,512]{1,0:T(8,128)S(1)}, u32[]{:S(2)}, u32[]{:S(2)}) collective-permute-start(f32[128,512]{1,0:T(8,128)} %collective-permute-done.9), channel_id=1, source_target_pairs={{0,4},{4,8},{8,12},{12,16},{16,20},{20,24},{24,28},{1,5},{5,9},{9,... | collective-permute-start | bytes 786440 | tf_op jit(solution)/shard_map/ppermute | solution.py:13
  81.9 4.0 %collective-permute-done.5 = f32[128,512]{1,0:T(8,128)S(1)} collective-permute-done((f32[128,512]{1,0:T(8,128)S(1)}, f32[128,512]{1,0:T(8,128)S(1)}, u32[]{:S(2)}, u32[]{:S(2)}) %collective-permute-start.5) | collective-permute-done | bytes 262176 | tf_op jit(solution)/shard_map/ppermute | solution.py:13
  87.4 1.9 %collective-permute-start.6 = (f32[128,512]{1,0:T(8,128)S(1)}, f32[128,512]{1,0:T(8,128)S(1)}, u32[]{:S(2)}, u32[]{:S(2)}) collective-permute-start(f32[128,512]{1,0:T(8,128)S(1)} %fusion.45), channel_id=1, source_target_pairs={{0,4},{4,8},{8,12},{12,16},{16,20},{20,24},{24,28},{1,5},{5,9},{9,... | collective-permute-start | bytes 786440 | tf_op jit(solution)/shard_map/ppermute | solution.py:13
  89.3 1.9 %collective-permute-start.11 = (f32[128,512]{1,0:T(8,128)S(1)}, f32[128,512]{1,0:T(8,128)}, u32[]{:S(2)}, u32[]{:S(2)}) collective-permute-start(f32[128,512]{1,0:T(8,128)S(1)} %collective-permute-done.10), channel_id=1, source_target_pairs={{0,4},{4,8},{8,12},{12,16},{16,20},{20,24},{24,28},{1,5},{5,9},{9,... | collective-permute-start | bytes 786440 | tf_op jit(solution)/shard_map/ppermute | solution.py:13
  91.2 4.7 %collective-permute-done.6 = f32[128,512]{1,0:T(8,128)S(1)} collective-permute-done((f32[128,512]{1,0:T(8,128)S(1)}, f32[128,512]{1,0:T(8,128)S(1)}, u32[]{:S(2)}, u32[]{:S(2)}) %collective-permute-start.6) | collective-permute-done | bytes 262176 | tf_op jit(solution)/shard_map/ppermute | solution.py:13
  97.4 1.9 %collective-permute-start.7 = (f32[128,512]{1,0:T(8,128)S(1)}, f32[128,512]{1,0:T(8,128)S(1)}, u32[]{:S(2)}, u32[]{:S(2)}) collective-permute-start(f32[128,512]{1,0:T(8,128)S(1)} %fusion.44), channel_id=1, source_target_pairs={{0,4},{4,8},{8,12},{12,16},{16,20},{20,24},{24,28},{1,5},{5,9},{9,... | collective-permute-start | bytes 786440 | tf_op jit(solution)/shard_map/ppermute | solution.py:13
  99.3 2.1 %collective-permute-start.12 = (f32[128,512]{1,0:T(8,128)}, f32[128,512]{1,0:T(8,128)S(1)}, u32[]{:S(2)}, u32[]{:S(2)}) collective-permute-start(f32[128,512]{1,0:T(8,128)} %collective-permute-done.11), channel_id=1, source_target_pairs={{0,4},{4,8},{8,12},{12,16},{16,20},{20,24},{24,28},{1,5},{5,9},{9,... | collective-permute-start | bytes 786440 | tf_op jit(solution)/shard_map/ppermute | solution.py:13
  101.4 4.6 %collective-permute-done.7 = f32[128,512]{1,0:T(8,128)S(1)} collective-permute-done((f32[128,512]{1,0:T(8,128)S(1)}, f32[128,512]{1,0:T(8,128)S(1)}, u32[]{:S(2)}, u32[]{:S(2)}) %collective-permute-start.7) | collective-permute-done | bytes 262176 | tf_op jit(solution)/shard_map/ppermute | solution.py:13
  108.9 6.8 %collective-permute-done.8 = f32[128,512]{1,0:T(8,128)S(1)} collective-permute-done((f32[128,512]{1,0:T(8,128)S(1)}, f32[128,512]{1,0:T(8,128)S(1)}, u32[]{:S(2)}, u32[]{:S(2)}) %collective-permute-start.8) | collective-permute-done | bytes 262176 | tf_op jit(solution)/shard_map/while/body/eval_jaxpr/ppermute | solution.py:13
  117.1 1.9 %collective-permute-start.13 = (f32[128,512]{1,0:T(8,128)S(1)}, f32[128,512]{1,0:T(8,128)S(1)}, u32[]{:S(2)}, u32[]{:S(2)}) collective-permute-start(f32[128,512]{1,0:T(8,128)S(1)} %fusion.42), channel_id=1, source_target_pairs={{0,4},{4,8},{8,12},{12,16},{16,20},{20,24},{24,28},{1,5},{5,9},{9,... | collective-permute-start | bytes 786440 | tf_op jit(solution)/shard_map/ppermute | solution.py:13
  119.0 6.7 %collective-permute-done.13 = f32[128,512]{1,0:T(8,128)S(1)} collective-permute-done((f32[128,512]{1,0:T(8,128)S(1)}, f32[128,512]{1,0:T(8,128)S(1)}, u32[]{:S(2)}, u32[]{:S(2)}) %collective-permute-start.13) | collective-permute-done | bytes 262176 | tf_op jit(solution)/shard_map/ppermute | solution.py:13
  127.1 1.9 %collective-permute-start.14 = (f32[128,512]{1,0:T(8,128)S(1)}, f32[128,512]{1,0:T(8,128)S(1)}, u32[]{:S(2)}, u32[]{:S(2)}) collective-permute-start(f32[128,512]{1,0:T(8,128)S(1)} %fusion.41), channel_id=1, source_target_pairs={{0,4},{4,8},{8,12},{12,16},{16,20},{20,24},{24,28},{1,5},{5,9},{9,... | collective-permute-start | bytes 786440 | tf_op jit(solution)/shard_map/ppermute | solution.py:13
  129.0 6.7 %collective-permute-done.14 = f32[128,512]{1,0:T(8,128)S(1)} collective-permute-done((f32[128,512]{1,0:T(8,128)S(1)}, f32[128,512]{1,0:T(8,128)S(1)}, u32[]{:S(2)}, u32[]{:S(2)}) %collective-permute-start.14) | collective-permute-done | bytes 262176 | tf_op jit(solution)/shard_map/ppermute | solution.py:13
  137.0 2.1 %collective-permute-start.15 = (f32[128,512]{1,0:T(8,128)S(1)}, f32[128,512]{1,0:T(8,128)S(1)}, u32[]{:S(2)}, u32[]{:S(2)}) collective-permute-start(f32[128,512]{1,0:T(8,128)S(1)} %fusion.40), channel_id=1, source_target_pairs={{0,4},{4,8},{8,12},{12,16},{16,20},{20,24},{24,28},{1,5},{5,9},{9,... | collective-permute-start | bytes 786440 | tf_op jit(solution)/shard_map/ppermute | solution.py:13
  139.1 6.5 %collective-permute-done.15 = f32[128,512]{1,0:T(8,128)S(1)} collective-permute-done((f32[128,512]{1,0:T(8,128)S(1)}, f32[128,512]{1,0:T(8,128)S(1)}, u32[]{:S(2)}, u32[]{:S(2)}) %collective-permute-start.15) | collective-permute-done | bytes 262176 | tf_op jit(solution)/shard_map/ppermute | solution.py:13
  149.5 1.6 fusion.11
  151.1 1.6 fusion.8
  152.7 1.6 fusion.5
  154.4 1.6 fusion.24
  156.3 2.4 %copy.51 = bf16[4,512,512]{2,1,0:T(8,128)(2,1)} copy(bf16[4,512,512]{1,2,0:T(8,128)(2,1)S(1)} %pad_maximum_fusion) | data formatting | bytes 4194304 | tf_op jit(solution)/shard_map/stack | solution.py:93
  (70 shorter events, 28.7 us)
Async XLA Ops:
  0.0 47.1 %copy-start.9 = (bf16[4,128,512]{2,1,0:T(8,128)(2,1)S(1)}, bf16[4,128,512]{2,1,0:T(8,128)(2,1)}, u32[]{:S(2)}) copy-start(bf16[4,128,512]{2,1,0:T(8,128)(2,1)} %param.3) | copy-start | bytes 1572868
  0.0 15.8 %collective-permute-start = (bf16[4,128,512]{2,1,0:T(8,128)(2,1)}, bf16[4,128,512]{2,1,0:T(8,128)(2,1)S(1)}, u32[]{:S(2)}, u32[]{:S(2)}) collective-permute-start(bf16[4,128,512]{2,1,0:T(8,128)(2,1)} %param.3), channel_id=1, source_target_pairs={{0,1},{1,2},{2,3},{3,0},{4,5},{5,6},{6,7},{7,4},{8,9},{9,10},{10,1... | collective-permute-start | bytes 1572872 | tf_op jit(solution)/shard_map/ppermute | solution.py:45
  15.8 14.8 %collective-permute-start.1 = (bf16[4,128,512]{2,1,0:T(8,128)(2,1)S(1)}, bf16[4,128,512]{2,1,0:T(8,128)(2,1)}, u32[]{:S(2)}, u32[]{:S(2)}) collective-permute-start(bf16[4,128,512]{2,1,0:T(8,128)(2,1)S(1)} %collective-permute-done), channel_id=1, source_target_pairs={{0,1},{1,2},{2,3},{3,0},{4,5},{5,6},{6,7},{7,4},{8,9},{9,10},{10,1... | collective-permute-start | bytes 1572872 | tf_op jit(solution)/shard_map/ppermute | solution.py:45
  30.7 14.2 %collective-permute-start.2 = (bf16[4,128,512]{2,1,0:T(8,128)(2,1)}, bf16[4,128,512]{2,1,0:T(8,128)(2,1)}, u32[]{:S(2)}, u32[]{:S(2)}) collective-permute-start(bf16[4,128,512]{2,1,0:T(8,128)(2,1)} %collective-permute-done.1), channel_id=1, source_target_pairs={{0,1},{1,2},{2,3},{3,0},{4,5},{5,6},{6,7},{7,4},{8,9},{9,10},{10,1... | collective-permute-start | bytes 1572872 | tf_op jit(solution)/shard_map/ppermute | solution.py:45
  33.1 16.3 %copy-start.1 = (f32[1,512,512]{2,1,0:T(8,128)S(1)}, f32[1,512,512]{2,1,0:T(8,128)}, u32[]{:S(2)}) copy-start(f32[1,512,512]{2,1,0:T(8,128)} %param.5) | copy-start | bytes 3145732
  49.4 2.0 %copy-start = (bf16[4,1024,512]{2,1,0:T(8,128)(2,1)}, bf16[4,1024,512]{2,1,0:T(8,128)(2,1)S(1)}, u32[]{:S(2)}) copy-start(bf16[4,1024,512]{2,1,0:T(8,128)(2,1)S(1)} %constant_dynamic-update-slice_fusion) | copy-start | bytes 12582916
  52.0 17.1 %collective-permute-start.4 = (f32[512,512]{0,1:T(8,128)S(1)}, f32[512,512]{0,1:T(8,128)}, u32[]{:S(2)}, u32[]{:S(2)}) collective-permute-start(f32[512,512]{0,1:T(8,128)S(1)} %fusion.15), channel_id=1, source_target_pairs={{0,4},{4,8},{8,12},{12,16},{16,20},{20,24},{24,28},{1,5},{5,9},{9,... | collective-permute-start | bytes 3145736 | tf_op jit(solution)/shard_map/ppermute | solution.py:13
  56.7 18.1 %collective-permute-start.3 = (f32[128,512]{1,0:T(8,128)}, f32[128,512]{1,0:T(8,128)}, u32[]{:S(2)}, u32[]{:S(2)}) collective-permute-start(f32[128,512]{1,0:T(8,128)} %get-tuple-element.33), channel_id=1, source_target_pairs={{0,4},{4,8},{8,12},{12,16},{16,20},{20,24},{24,28},{1,5},{5,9},{9,... | collective-permute-start | bytes 786440 | tf_op jit(solution)/shard_map/ppermute | solution.py:13
  60.7 18.6 %collective-permute-start.9 = (f32[128,512]{1,0:T(8,128)}, f32[128,512]{1,0:T(8,128)}, u32[]{:S(2)}, u32[]{:S(2)}) collective-permute-start(f32[128,512]{1,0:T(8,128)} %get-tuple-element.32), channel_id=1, source_target_pairs={{0,4},{4,8},{8,12},{12,16},{16,20},{20,24},{24,28},{1,5},{5,9},{9,... | collective-permute-start | bytes 786440 | tf_op jit(solution)/shard_map/ppermute | solution.py:13
  74.8 22.6 %copy-start.2 = (f32[128,1,512]{2,1,0:T(1,128)}, f32[128,1,512]{2,1,0:T(1,128)S(1)}, u32[]{:S(2)}) copy-start(f32[128,1,512]{2,1,0:T(1,128)S(1)} %get-tuple-element.20) | copy-start | bytes 786436
  74.8 22.6 %copy-start.4 = (f32[128,1,512]{2,1,0:T(1,128)}, f32[128,1,512]{2,1,0:T(1,128)S(1)}, u32[]{:S(2)}) copy-start(f32[128,1,512]{2,1,0:T(1,128)S(1)} %get-tuple-element.28) | copy-start | bytes 786436
  74.8 22.6 %copy-start.6 = (f32[128,1,512]{2,1,0:T(1,128)}, f32[128,1,512]{2,1,0:T(1,128)S(1)}, u32[]{:S(2)}) copy-start(f32[128,1,512]{2,1,0:T(1,128)S(1)} %get-tuple-element.30) | copy-start | bytes 786436
  74.8 31.2 %copy-start.8 = (f32[128,1,512]{2,1,0:T(1,128)S(1)}, f32[128,1,512]{2,1,0:T(1,128)}, u32[]{:S(2)}) copy-start(f32[128,1,512]{2,1,0:T(1,128)} %get-tuple-element.19) | copy-start | bytes 786436
  77.4 8.6 %collective-permute-start.5 = (f32[128,512]{1,0:T(8,128)S(1)}, f32[128,512]{1,0:T(8,128)S(1)}, u32[]{:S(2)}, u32[]{:S(2)}) collective-permute-start(f32[128,512]{1,0:T(8,128)S(1)} %fusion.46), channel_id=1, source_target_pairs={{0,4},{4,8},{8,12},{12,16},{16,20},{20,24},{24,28},{1,5},{5,9},{9,... | collective-permute-start | bytes 786440 | tf_op jit(solution)/shard_map/ppermute | solution.py:13
  79.3 10.0 %collective-permute-start.10 = (f32[128,512]{1,0:T(8,128)}, f32[128,512]{1,0:T(8,128)S(1)}, u32[]{:S(2)}, u32[]{:S(2)}) collective-permute-start(f32[128,512]{1,0:T(8,128)} %collective-permute-done.9), channel_id=1, source_target_pairs={{0,4},{4,8},{8,12},{12,16},{16,20},{20,24},{24,28},{1,5},{5,9},{9,... | collective-permute-start | bytes 786440 | tf_op jit(solution)/shard_map/ppermute | solution.py:13
  87.4 8.6 %collective-permute-start.6 = (f32[128,512]{1,0:T(8,128)S(1)}, f32[128,512]{1,0:T(8,128)S(1)}, u32[]{:S(2)}, u32[]{:S(2)}) collective-permute-start(f32[128,512]{1,0:T(8,128)S(1)} %fusion.45), channel_id=1, source_target_pairs={{0,4},{4,8},{8,12},{12,16},{16,20},{20,24},{24,28},{1,5},{5,9},{9,... | collective-permute-start | bytes 786440 | tf_op jit(solution)/shard_map/ppermute | solution.py:13
  89.3 10.0 %collective-permute-start.11 = (f32[128,512]{1,0:T(8,128)S(1)}, f32[128,512]{1,0:T(8,128)}, u32[]{:S(2)}, u32[]{:S(2)}) collective-permute-start(f32[128,512]{1,0:T(8,128)S(1)} %collective-permute-done.10), channel_id=1, source_target_pairs={{0,4},{4,8},{8,12},{12,16},{16,20},{20,24},{24,28},{1,5},{5,9},{9,... | collective-permute-start | bytes 786440 | tf_op jit(solution)/shard_map/ppermute | solution.py:13
  97.4 8.6 %collective-permute-start.7 = (f32[128,512]{1,0:T(8,128)S(1)}, f32[128,512]{1,0:T(8,128)S(1)}, u32[]{:S(2)}, u32[]{:S(2)}) collective-permute-start(f32[128,512]{1,0:T(8,128)S(1)} %fusion.44), channel_id=1, source_target_pairs={{0,4},{4,8},{8,12},{12,16},{16,20},{20,24},{24,28},{1,5},{5,9},{9,... | collective-permute-start | bytes 786440 | tf_op jit(solution)/shard_map/ppermute | solution.py:13
  99.3 26.4 %copy-start.7 = (f32[128,1,512]{2,1,0:T(1,128)S(1)}, f32[128,1,512]{2,1,0:T(1,128)}, u32[]{:S(2)}) copy-start(f32[128,1,512]{2,1,0:T(1,128)} %copy-done.6) | copy-start | bytes 786436
  99.3 36.4 %copy-start.5 = (f32[128,1,512]{2,1,0:T(1,128)S(1)}, f32[128,1,512]{2,1,0:T(1,128)}, u32[]{:S(2)}) copy-start(f32[128,1,512]{2,1,0:T(1,128)} %copy-done.4) | copy-start | bytes 786436
  99.3 9.5 %collective-permute-start.12 = (f32[128,512]{1,0:T(8,128)}, f32[128,512]{1,0:T(8,128)S(1)}, u32[]{:S(2)}, u32[]{:S(2)}) collective-permute-start(f32[128,512]{1,0:T(8,128)} %collective-permute-done.11), channel_id=1, source_target_pairs={{0,4},{4,8},{8,12},{12,16},{16,20},{20,24},{24,28},{1,5},{5,9},{9,... | collective-permute-start | bytes 786440 | tf_op jit(solution)/shard_map/ppermute | solution.py:13
  107.2 38.4 %copy-start.3 = (f32[128,1,512]{2,1,0:T(1,128)S(1)}, f32[128,1,512]{2,1,0:T(1,128)}, u32[]{:S(2)}) copy-start(f32[128,1,512]{2,1,0:T(1,128)} %copy-done.2) | copy-start | bytes 786436
  107.3 8.4 %collective-permute-start.8 = (f32[128,512]{1,0:T(8,128)S(1)}, f32[128,512]{1,0:T(8,128)S(1)}, u32[]{:S(2)}, u32[]{:S(2)}) collective-permute-start(f32[128,512]{1,0:T(8,128)S(1)} %fusion.43), channel_id=1, source_target_pairs={{0,16},{4,20},{8,24},{12,28},{1,17},{5,21},{9,25},{13,29},{2,18},{... | collective-permute-start | bytes 786440 | tf_op jit(solution)/shard_map/while/body/eval_jaxpr/ppermute | solution.py:13
  117.1 8.6 %collective-permute-start.13 = (f32[128,512]{1,0:T(8,128)S(1)}, f32[128,512]{1,0:T(8,128)S(1)}, u32[]{:S(2)}, u32[]{:S(2)}) collective-permute-start(f32[128,512]{1,0:T(8,128)S(1)} %fusion.42), channel_id=1, source_target_pairs={{0,4},{4,8},{8,12},{12,16},{16,20},{20,24},{24,28},{1,5},{5,9},{9,... | collective-permute-start | bytes 786440 | tf_op jit(solution)/shard_map/ppermute | solution.py:13
  127.1 8.6 %collective-permute-start.14 = (f32[128,512]{1,0:T(8,128)S(1)}, f32[128,512]{1,0:T(8,128)S(1)}, u32[]{:S(2)}, u32[]{:S(2)}) collective-permute-start(f32[128,512]{1,0:T(8,128)S(1)} %fusion.41), channel_id=1, source_target_pairs={{0,4},{4,8},{8,12},{12,16},{16,20},{20,24},{24,28},{1,5},{5,9},{9,... | collective-permute-start | bytes 786440 | tf_op jit(solution)/shard_map/ppermute | solution.py:13
  137.0 8.6 %collective-permute-start.15 = (f32[128,512]{1,0:T(8,128)S(1)}, f32[128,512]{1,0:T(8,128)S(1)}, u32[]{:S(2)}, u32[]{:S(2)}) collective-permute-start(f32[128,512]{1,0:T(8,128)S(1)} %fusion.40), channel_id=1, source_target_pairs={{0,4},{4,8},{8,12},{12,16},{16,20},{20,24},{24,28},{1,5},{5,9},{9,... | collective-permute-start | bytes 786440 | tf_op jit(solution)/shard_map/ppermute | solution.py:13
